TPU v7x, 32 devices: a whole 2x2x4 slice. The times are simulated.
32 devices in a mesh: dp: 8 (over y, x, core), mp: 4 (over z).
Axes of the slice: x: 2, y: 2, z: 4, core: 2. Of those that a mesh axis runs over, the one named last changes fastest.
Arguments:
- feature_ids: int32 [8, 2048, 8], P('dp'), may hold values from 0 to 4095
- tables: bfloat16 [8, 4096, 128], P('dp'), may hold values from -5 to 5
- table_of_feature: int32 [8], replicated, may hold values from 0 to 7, each once
- cross_down: bfloat16 [2, 1024, 512], P(None, 'mp'), may hold values from -0.1875 to 0.1875
- cross_up: bfloat16 [2, 1024, 512], P(None, 'mp'), may hold values from -0.125 to 0.125
- cross_bias: float32 [2, 1024], P(None, 'mp'), may hold values from -3 to 3
- tower_weight: bfloat16 [1024, 2048], P('dp', 'mp'), may hold values from -0.1875 to 0.1875
- tower_bias: float32 [2048], P('mp'), may hold values from -3 to 3
Outputs:
- hidden: bfloat16 [2048, 2048], P('dp', 'mp')
Inputs may be any that keep to these rules, and one draw needn't show every extreme that they name: `feature_ids`: each id indexes a row of its own table. `table_of_feature`: each table serves exactly one feature.
All inputs are finite; a program needn't handle non-finite values.
Results may differ from a plain program's by a relative error of at most 0.015.
Values may be sent and summed in bfloat16 or wider, within the bound.
A program may use at most 64 MiB of HBM per device.

v0:
```python
import jax
import jax.numpy as jnp
from jax import lax
from jax.sharding import PartitionSpec as P


def body(
    feature_ids,
    tables,
    table_of_feature,
    cross_down,
    cross_up,
    cross_bias,
    tower_weight,
    tower_bias,
):
    groups = lax.axis_size("dp")
    members = lax.axis_size("mp")
    member = lax.axis_index("mp")
    table_count, batch_size, hot_count = feature_ids.shape
    row_count = batch_size // (groups * members)
    shaped = feature_ids[0].reshape(groups, members, row_count, hot_count)
    own_ids = lax.dynamic_index_in_dim(shaped, member, 1, keepdims=False).reshape(
        groups * row_count, hot_count
    )
    summed = jnp.zeros((groups * row_count, tables.shape[2]), jnp.float32)
    for hot_index in range(hot_count):
        summed = summed + jnp.take(tables[0], own_ids[:, hot_index], axis=0).astype(jnp.float32)
    columns = [summed.astype(jnp.bfloat16)]
    pooled = jnp.stack(columns, axis=1)
    regrouped = lax.all_to_all(pooled, "dp", split_axis=0, concat_axis=1, tiled=True)
    ordered = jnp.take(regrouped, table_of_feature, axis=1)
    by_width = lax.all_to_all(ordered, "mp", split_axis=1, concat_axis=0, tiled=True)
    group_rows = by_width.shape[0]
    embedded = by_width.reshape(group_rows, -1)
    embedded_wide = embedded.astype(jnp.float32)
    crossed = embedded
    layer_total = cross_down.shape[0]
    for layer_index in range(layer_total):
        partial_value = jnp.dot(
            crossed, cross_down[layer_index], preferred_element_type=jnp.float32
        )
        projected = lax.psum(partial_value.astype(jnp.bfloat16), "mp")
        lifted = lax.dot_general(
            projected,
            cross_up[layer_index],
            (((1,), (1,)), ((), ())),
            preferred_element_type=jnp.float32,
        )
        crossed = (
            embedded_wide * (lifted + cross_bias[layer_index]) + crossed.astype(jnp.float32)
        ).astype(jnp.bfloat16)
    full_rows = lax.all_gather(crossed, "mp", axis=1, tiled=True)
    pre_act = jnp.dot(
        full_rows,
        lax.all_gather(tower_weight, "dp", axis=0, tiled=True),
        preferred_element_type=jnp.float32,
    )
    return jax.nn.relu(pre_act + tower_bias).astype(jnp.bfloat16)


def solution(mesh):
    return jax.shard_map(
        body,
        mesh=mesh,
        in_specs=(
            P("dp", None, None),
            P("dp", None, None),
            P(),
            P(None, "mp", None),
            P(None, "mp", None),
            P(None, "mp"),
            P("dp", "mp"),
            P("mp"),
        ),
        out_specs=P("dp", "mp"),
        check_vma=False,
    )
```

profile of v0, /device:TPU:0, one launch (start us, length us, event | category | flops | bytes accessed | tf_op | source)
XLA Modules:
  0.0 143.6 jit_solution(9518459660529289800)
XLA Ops:
  7.4 1.0 reshape_squeeze.3
  8.8 1.3 gather_fusion.2
  10.2 1.3 gather_fusion.3
  11.5 1.3 gather_fusion.4
  12.9 1.3 gather_fusion.5
  14.2 1.3 gather_fusion.6
  15.6 1.3 gather_fusion.7
  17.0 1.3 gather_fusion.8
  18.3 1.3 gather_fusion.1
  19.7 0.8 fusion.16
  21.0 0.7 reduce.4
  21.7 0.7 reshape.125
  22.3 5.3 %all-to-all-start = ((bf16[8,2,4096]{2,1,0:T(2,128)(2,1)}), bf16[8,2,4096]{2,1,0:T(2,128)(2,1)S(1)}, u32[]{:S(2)}, u32[]{:S(2)}) async-start(bf16[8,2,4096]{2,1,0:T(2,128)(2,1)} %reshape.125), calls=%async_computation | async-start | bytes 262144 | tf_op jit(solution)/shard_map/all_to_all | solution.py:31
  27.8 5.4 %all-to-all-done = bf16[8,2,4096]{2,1,0:T(2,128)(2,1)S(1)} async-done(((bf16[8,2,4096]{2,1,0:T(2,128)(2,1)}), bf16[8,2,4096]{2,1,0:T(2,128)(2,1)S(1)}, u32[]{:S(2)}, u32[]{:S(2)}) %all-to-all-start) | async-done | bytes 131104 | tf_op jit(solution)/shard_map/all_to_all | solution.py:31
  34.0 10.6 %all_to_all.33 = bf16[64,8,128]{2,0,1:T(8,128)(2,1)S(1)} all-to-all(bf16[64,8,128]{2,0,1:T(8,128)(2,1)S(1)} %select_bitcast_fusion), channel_id=1, replica_groups=mesh['dp'=8,'mp'=4] {'mp'}, dimensions={1} | all-to-all | bytes 262144 | tf_op jit(solution)/shard_map/all_to_all | solution.py:33
  44.8 0.9 convolution_convert_fusion.1
  45.8 0.6 copy-done.2
  46.4 32.4 %all-reduce.3.cloned.1.call-done = bf16[256,512]{1,0:T(8,128)(2,1)} async-done(((bf16[256,512]{1,0:T(8,128)(2,1)}), bf16[256,512]{1,0:T(8,128)(2,1)}) %all-reduce.3.cloned.1.call-update) | async-done | bytes 262160 | tf_op jit(solution)/shard_map/psum | solution.py:43
  78.8 1.2 fusion.6
  80.0 0.9 convolution_convert_fusion
  81.5 35.1 %all-reduce.5.cloned.1.call-done = bf16[256,512]{1,0:T(8,128)(2,1)} async-done(((bf16[256,512]{1,0:T(8,128)(2,1)}), bf16[256,512]{1,0:T(8,128)(2,1)}) %all-reduce.5.cloned.1.call-update) | async-done | bytes 262160 | tf_op jit(solution)/shard_map/psum | solution.py:43
  116.6 1.2 fusion.7
  117.8 16.0 %all_gather.6 = bf16[256,1024]{1,0:T(8,128)(2,1)S(1)} all-gather(bf16[256,256]{1,0:T(8,128)(2,1)S(1)} %fusion.7), channel_id=1, replica_groups=mesh['dp'=8,'mp'=4] {'mp'}, dimensions={1}, use_global_device_ids=true | all-gather | bytes 655360 | tf_op jit(solution)/shard_map/all_gather | solution.py:53
  133.8 2.4 %fusion.1 = bf16[256,512]{1,0:T(8,128)(2,1)} fusion(bf16[256,1024]{1,0:T(8,128)(2,1)S(1)} %all_gather.6, bf16[1024,512]{1,0:T(8,128)(2,1)} %all-gather.2.cloned.1.call-done, f32[512]{0:T(512)S(1)} %copy-done.4), kind=kOutput, calls=%fused_computation.11 | convolution fusion | flops 268828672 | bytes 1837056 | tf_op jit(solution)/shard_map/dot_general | solution.py:54
  (51 shorter events, 2.5 us)
Async XLA Ops:
  7.4 1.4 %copy-start = (bf16[1,4096,128]{2,1,0:T(8,128)(2,1)S(1)}, bf16[1,4096,128]{2,1,0:T(8,128)(2,1)}, u32[]{:S(2)}) copy-start(bf16[1,4096,128]{2,1,0:T(8,128)(2,1)} %param.11) | copy-start | bytes 3145732
  22.3 5.4 %copy-start.5 = (s32[8]{0:T(128)S(1)}, s32[8]{0:T(128)}, u32[]{:S(2)}) copy-start(s32[8]{0:T(128)} %param.12) | copy-start | bytes 100
  22.3 10.8 %all-to-all-start = ((bf16[8,2,4096]{2,1,0:T(2,128)(2,1)}), bf16[8,2,4096]{2,1,0:T(2,128)(2,1)S(1)}, u32[]{:S(2)}, u32[]{:S(2)}) async-start(bf16[8,2,4096]{2,1,0:T(2,128)(2,1)} %reshape.125), calls=%async_computation | async-start | bytes 262144 | tf_op jit(solution)/shard_map/all_to_all | solution.py:31
  27.7 51.1 %all-reduce.3.cloned.1.call-start = ((), (), s32[]{:S(2)}) async-start(), calls=%async_computation.2 | async-start | bytes 524288 | tf_op jit(solution)/shard_map/psum | solution.py:43
  33.3 11.5 %copy-start.1 = (bf16[2,256,512]{2,1,0:T(8,128)(2,1)S(1)}, bf16[2,256,512]{2,1,0:T(8,128)(2,1)}, u32[]{:S(2)}) copy-start(bf16[2,256,512]{2,1,0:T(8,128)(2,1)} %param.13) | copy-start | bytes 1572868
  44.8 34.0 %copy-start.3 = (bf16[2,256,512]{2,1,0:T(8,128)(2,1)S(1)}, bf16[2,256,512]{2,1,0:T(8,128)(2,1)}, u32[]{:S(2)}) copy-start(bf16[2,256,512]{2,1,0:T(8,128)(2,1)} %param.14) | copy-start | bytes 1572868
  45.7 0.7 copy-start.2
  45.8 70.8 %all-reduce.5.cloned.1.call-start = ((), (), s32[]{:S(2)}) async-start(), calls=%async_computation.3 | async-start | bytes 524288 | tf_op jit(solution)/shard_map/psum | solution.py:43
  81.0 52.8 %all-gather.2.cloned.1.call-start = ((), (), s32[]{:S(2)}) async-start(), calls=%async_computation.4 | async-start | bytes 1179648 | tf_op jit(solution)/shard_map/all_gather | solution.py:56
  117.8 16.0 %copy-start.4 = (f32[512]{0:T(512)S(1)}, f32[512]{0:T(512)}, u32[]{:S(2)}) copy-start(f32[512]{0:T(512)} %param.17) | copy-start | bytes 6148
Sparse Core Ops, SparseCore 0:
  45.9 32.8 all-reduce.2
  81.1 35.4 all-reduce.4
Sparse Core Ops, SparseCore 1:
  83.3 23.1 all-gather.1
where the time goes:
time: 144 us
  waiting for transfers between devices  73.4 us (51%)
  blocking collectives  26.6 us (18%)
  between operations  15.2 us (11%)
  local copies, waits for them, and re-layouts  14.7 us (10%)
  matrix products  6.65 us (5%)
  starting transfers between devices  5.45 us (4%)
  other arithmetic  1.66 us (1%)
    psum x2, waiting for transfers between devices, body(): projected = lax.psum(partial_value.astype(jnp.bfloat16), 'mp')  67.4 us
    all_gather x1, blocking collectives, body(): full_rows = lax.all_gather(crossed, 'mp', axis=1, tiled=True)  16 us
    gather x8, local copies, waits for them, and re-layouts, body(): jnp.take(tables[0], own_ids[:, hot_index], axis=0).astype(jnp.float32)  10.7 us
    all_to_all x1, blocking collectives, body(): lax.all_to_all(ordered, 'mp', split_axis=1, concat_axis=0, tiled=True)  10.6 us
    all_to_all x1, waiting for transfers between devices, body(): lax.all_to_all(pooled, 'dp', split_axis=0, concat_axis=1, tiled=True)  5.4 us
    all_to_all x1, starting transfers between devices, body(): lax.all_to_all(pooled, 'dp', split_axis=0, concat_axis=1, tiled=True)  5.33 us
  transfers between devices with their start and end apart: 4, of which 3 were waited for; matrix products, arithmetic and copies ran while one was open for 1% of the time, Pallas kernels for 0%

commit v1 on v0

--- a/solution.py
+++ b/solution.py
@@ -40,7 +40,7 @@
         partial_value = jnp.dot(
             crossed, cross_down[layer_index], preferred_element_type=jnp.float32
         )
-        projected = lax.psum(partial_value.astype(jnp.bfloat16), "mp")
+        projected = jnp.sum(lax.all_gather(partial_value.astype(jnp.bfloat16), "mp"), axis=0)
         lifted = lax.dot_general(
             projected,
             cross_up[layer_index],

time: 144 us -> 135 us (0.938)
  waiting for transfers between devices: 73.4 us -> 65.3 us
  other arithmetic: 1.66 us -> 4.62 us
  matrix products: 6.65 us -> 4.76 us
  between operations: 15.2 us -> 13.5 us
    psum x2 -> x0, waiting for transfers between devices: 67.4 us -> none  [body(): projected = lax.psum(partial_value.astype(jnp.bfloat16), 'mp')]
    all_gather x0 -> x2, waiting for transfers between devices: none -> 51.5 us  [body(): lax.all_gather(partial_value.astype(jnp.bfloat16), 'mp')]
    all_gather x1, waiting for transfers between devices: 0.01 us -> 7.64 us  [body(): lax.all_gather(tower_weight, 'dp', axis=0, tiled=True)]
    reduce_sum x0 -> x2, other arithmetic: none -> 2.96 us  [body(): jnp.sum(lax.all_gather(partial_value.astype(jnp.bfloat16), 'mp'), axis=0)]
    dot_general x2, matrix products: 2.42 us -> 0.52 us  [body(): lax.dot_general(projected, cross_up[layer_index], (((1,), (1,)), ((), ())...]
  transfers between devices with their start and end apart: 4 -> 4, of which waited for: 3 -> 4; matrix products, arithmetic and copies ran while one was open for 1% -> 1% of each run, Pallas kernels for 0% -> 0%
where the time goes in v1:
time: 135 us; the launch traced here: 134 us
  waiting for transfers between devices  65.3 us (48%)
  blocking collectives  25.9 us (19%)
  local copies, waits for them, and re-layouts  14.6 us (11%)
  between operations  13.5 us (10%)
  starting transfers between devices  5.45 us (4%)
  matrix products  4.76 us (4%)
  other arithmetic  4.62 us (3%)
    all_gather x2, waiting for transfers between devices, body(): lax.all_gather(partial_value.astype(jnp.bfloat16), 'mp')  51.5 us
    all_gather x1, blocking collectives, body(): full_rows = lax.all_gather(crossed, 'mp', axis=1, tiled=True)  15.3 us
    gather x8, local copies, waits for them, and re-layouts, body(): jnp.take(tables[0], own_ids[:, hot_index], axis=0).astype(jnp.float32)  10.7 us
    all_to_all x1, blocking collectives, body(): lax.all_to_all(ordered, 'mp', split_axis=1, concat_axis=0, tiled=True)  10.6 us
    all_gather x1, waiting for transfers between devices, body(): lax.all_gather(tower_weight, 'dp', axis=0, tiled=True)  7.64 us
    all_to_all x1, waiting for transfers between devices, body(): lax.all_to_all(pooled, 'dp', split_axis=0, concat_axis=1, tiled=True)  5.4 us
    all_to_all x1, starting transfers between devices, body(): lax.all_to_all(pooled, 'dp', split_axis=0, concat_axis=1, tiled=True)  5.33 us
    reduce_sum x2, other arithmetic, body(): jnp.sum(lax.all_gather(partial_value.astype(jnp.bfloat16), 'mp'), axis=0)  2.96 us
  transfers between devices with their start and end apart: 4, of which 4 were waited for; matrix products, arithmetic and copies ran while one was open for 1% of the time, Pallas kernels for 0%

profile of v1, /device:TPU:0, one launch (start us, length us, event | category | flops | bytes accessed | tf_op | source)
XLA Modules:
  0.0 134.2 jit_solution(10612441284163100651)
XLA Ops:
  6.5 1.0 reshape_squeeze.3
  8.0 1.3 gather_fusion.2
  9.3 1.3 gather_fusion.3
  10.7 1.3 gather_fusion.4
  12.1 1.3 gather_fusion.5
  13.4 1.3 gather_fusion.6
  14.8 1.3 gather_fusion.7
  16.1 1.3 gather_fusion.8
  17.5 1.3 gather_fusion.1
  18.9 0.8 fusion.16
  20.8 0.7 reshape.127
  21.5 5.3 %all-to-all-start = ((bf16[8,2,4096]{2,1,0:T(2,128)(2,1)}), bf16[8,2,4096]{2,1,0:T(2,128)(2,1)S(1)}, u32[]{:S(2)}, u32[]{:S(2)}) async-start(bf16[8,2,4096]{2,1,0:T(2,128)(2,1)} %reshape.127), calls=%async_computation | async-start | bytes 262144 | tf_op jit(solution)/shard_map/all_to_all | solution.py:31
  26.9 5.4 %all-to-all-done = bf16[8,2,4096]{2,1,0:T(2,128)(2,1)S(1)} async-done(((bf16[8,2,4096]{2,1,0:T(2,128)(2,1)}), bf16[8,2,4096]{2,1,0:T(2,128)(2,1)S(1)}, u32[]{:S(2)}, u32[]{:S(2)}) %all-to-all-start) | async-done | bytes 131104 | tf_op jit(solution)/shard_map/all_to_all | solution.py:31
  33.2 10.6 %all_to_all.33 = bf16[64,8,128]{2,0,1:T(8,128)(2,1)S(1)} all-to-all(bf16[64,8,128]{2,0,1:T(8,128)(2,1)S(1)} %select_bitcast_fusion), channel_id=1, replica_groups=mesh['dp'=8,'mp'=4] {'mp'}, dimensions={1} | all-to-all | bytes 262144 | tf_op jit(solution)/shard_map/all_to_all | solution.py:33
  44.0 0.9 convolution_convert_fusion.1
  45.6 24.7 %all-gather.8.cloned.1.call-done = bf16[1024,512]{1,0:T(8,128)(2,1)} async-done(((bf16[256,512]{1,0:T(8,128)(2,1)}), bf16[1024,512]{1,0:T(8,128)(2,1)}) %all-gather.8.cloned.1.call-update) | async-done | bytes 1048592 | tf_op jit(solution)/shard_map/all_gather | solution.py:43
  70.3 1.5 %reduce_sum.24 = bf16[256,512]{1,0:T(8,128)(2,1)S(1)} reduce(bf16[4,256,512]{2,1,0:T(8,128)(2,1)} %bitcast.62, bf16[]{:T(256)} %constant.40.clone.1), dimensions={0}, to_apply=%region_0.2 | reduce | flops 393216 | bytes 1310722 | tf_op jit(solution)/shard_map/reduce_sum | solution.py:43
  72.1 0.9 convolution_convert_fusion
  73.1 0.7 all-gather.6.cloned.1.call-update
  73.8 26.8 %all-gather.10.cloned.1.call-done = bf16[1024,512]{1,0:T(8,128)(2,1)} async-done(((bf16[256,512]{1,0:T(8,128)(2,1)}), bf16[1024,512]{1,0:T(8,128)(2,1)}) %all-gather.10.cloned.1.call-update) | async-done | bytes 1048592 | tf_op jit(solution)/shard_map/all_gather | solution.py:43
  100.6 1.5 %reduce_sum.25 = bf16[256,512]{1,0:T(8,128)(2,1)S(1)} reduce(bf16[4,256,512]{2,1,0:T(8,128)(2,1)} %bitcast.61, bf16[]{:T(256)} %constant.40.clone.1), dimensions={0}, to_apply=%region_1.3 | reduce | flops 393216 | bytes 1310722 | tf_op jit(solution)/shard_map/reduce_sum | solution.py:43
  102.3 15.3 %all_gather.22 = bf16[256,1024]{1,0:T(8,128)(2,1)S(1)} all-gather(bf16[256,256]{1,0:T(8,128)(2,1)S(1)} %fusion.7), channel_id=1, replica_groups=mesh['dp'=8,'mp'=4] {'mp'}, dimensions={1}, use_global_device_ids=true | all-gather | bytes 655360 | tf_op jit(solution)/shard_map/all_gather | solution.py:53
  117.6 7.6 %all-gather.6.cloned.1.call-done = bf16[1024,512]{1,0:T(8,128)(2,1)} async-done(((bf16[128,512]{1,0:T(8,128)(2,1)}), bf16[1024,512]{1,0:T(8,128)(2,1)}) %all-gather.6.cloned.1.call-update) | async-done | bytes 1048592 | tf_op jit(solution)/shard_map/all_gather | solution.py:56
  125.3 2.4 %fusion.1 = bf16[256,512]{1,0:T(8,128)(2,1)} fusion(bf16[256,1024]{1,0:T(8,128)(2,1)S(1)} %all_gather.22, bf16[1024,512]{1,0:T(8,128)(2,1)} %all-gather.6.cloned.1.call-done, f32[512]{0:T(512)S(1)} %copy-done.4), kind=kOutput, calls=%fused_computation.11 | convolution fusion | flops 268828672 | bytes 1837056 | tf_op jit(solution)/shard_map/dot_general | solution.py:54
  (53 shorter events, 3.7 us)
Async XLA Ops:
  6.5 1.4 %copy-start = (bf16[1,4096,128]{2,1,0:T(8,128)(2,1)S(1)}, bf16[1,4096,128]{2,1,0:T(8,128)(2,1)}, u32[]{:S(2)}) copy-start(bf16[1,4096,128]{2,1,0:T(8,128)(2,1)} %param.11) | copy-start | bytes 3145732
  21.5 5.4 %copy-start.5 = (s32[8]{0:T(128)S(1)}, s32[8]{0:T(128)}, u32[]{:S(2)}) copy-start(s32[8]{0:T(128)} %param.12) | copy-start | bytes 100
  21.5 10.8 %all-to-all-start = ((bf16[8,2,4096]{2,1,0:T(2,128)(2,1)}), bf16[8,2,4096]{2,1,0:T(2,128)(2,1)S(1)}, u32[]{:S(2)}, u32[]{:S(2)}) async-start(bf16[8,2,4096]{2,1,0:T(2,128)(2,1)} %reshape.127), calls=%async_computation | async-start | bytes 262144 | tf_op jit(solution)/shard_map/all_to_all | solution.py:31
  26.8 43.5 %all-gather.8.cloned.1.call-start = ((), (), s32[]{:S(2)}) async-start(), calls=%async_computation.3 | async-start | bytes 1310720 | tf_op jit(solution)/shard_map/all_gather | solution.py:43
  32.5 11.5 %copy-start.1 = (bf16[2,256,512]{2,1,0:T(8,128)(2,1)S(1)}, bf16[2,256,512]{2,1,0:T(8,128)(2,1)}, u32[]{:S(2)}) copy-start(bf16[2,256,512]{2,1,0:T(8,128)(2,1)} %param.13) | copy-start | bytes 1572868
  44.9 0.7 copy-start.2
  44.9 55.7 %all-gather.10.cloned.1.call-start = ((), (), s32[]{:S(2)}) async-start(), calls=%async_computation.4 | async-start | bytes 1310720 | tf_op jit(solution)/shard_map/all_gather | solution.py:43
  70.3 1.5 %copy-start.3 = (bf16[2,256,512]{2,1,0:T(8,128)(2,1)S(1)}, bf16[2,256,512]{2,1,0:T(8,128)(2,1)}, u32[]{:S(2)}) copy-start(bf16[2,256,512]{2,1,0:T(8,128)(2,1)} %param.14) | copy-start | bytes 1572868
  73.1 52.2 %all-gather.6.cloned.1.call-start = ((), (), s32[]{:S(2)}) async-start(), calls=%async_computation.2 | async-start | bytes 1179648 | tf_op jit(solution)/shard_map/all_gather | solution.py:56
  102.3 23.0 %copy-start.4 = (f32[512]{0:T(512)S(1)}, f32[512]{0:T(512)}, u32[]{:S(2)}) copy-start(f32[512]{0:T(512)} %param.17) | copy-start | bytes 6148
Sparse Core Ops, SparseCore 0:
  45.0 25.2 all-gather.7
  73.2 27.3 all-gather.9
  102.5 22.7 all-gather.5
